TPU v7x, 32 devices: a whole 2x2x4 slice. The times are simulated.
32 devices in a mesh: row: 4 (over x, core), col: 8 (over z, y).
Axes of the slice: x: 2, y: 2, z: 4, core: 2. Of those that a mesh axis runs over, the one named last changes fastest.
Arguments:
- panel_rows: float32 [4096, 4096], P('row', 'col'), may hold values from -0.75 to 0.75
- owner_slot: int32 [8, 8], replicated, may hold values from -1 to 15, as said below
Outputs:
- packed: float32 [4, 16, 512, 512], P('row', 'col')
Inputs may be any that keep to these rules, and one draw needn't show every extreme that they name: For j <= i, owner_slot[i, j] is the position of tile (i, j) among the 16 positions of group i // 2; tiles of one group have distinct positions; entries above the diagonal are -1. Position p lies on the device of col index p // 2.
All inputs are finite; a program needn't handle non-finite values.
Results may differ from a plain program's by a relative error of at most 0.0003.
Values sent between devices are 32-bit elements; how exact they have to be, the bound alone decides.
A program may use at most 128 MiB of HBM per device.

v0:
```python
import functools

import jax
import jax.numpy as jnp
from jax import lax
from jax.experimental import pallas as pl
from jax.experimental.pallas import tpu as pltpu
from jax.sharding import PartitionSpec as P

BLOCK = 512
EDGES = (0, 128, 256, 384, 512)
MESH = pl.DeviceIdType.MESH
NT = (((1,), (1,)), ((), ()))


def slot_table(owner_slot, group_id, positions, per_group):
    blocks = owner_slot.shape[0]
    block_row = jnp.arange(blocks, dtype=jnp.int32)[:, None]
    block_col = jnp.arange(blocks, dtype=jnp.int32)[None, :]
    inside = (block_row // per_group == group_id) & (block_col <= block_row)
    wanted = jnp.arange(positions, dtype=jnp.int32)[:, None, None]
    matched = inside[None] & (owner_slot[None] == wanted)
    is_live = jnp.any(matched, axis=(1, 2))
    left_block = jnp.sum(jnp.where(matched, block_row[None], 0), axis=(1, 2))
    right_block = jnp.sum(jnp.where(matched, block_col[None], 0), axis=(1, 2))
    return (left_block, right_block, is_live)


STAGES = len(EDGES) - 1
PIECES = []
for stage in range(STAGES):
    PIECES.append((stage, EDGES[stage], EDGES[stage + 1], 0, EDGES[stage + 1]))
    if stage:
        PIECES.append((stage, 0, EDGES[stage], EDGES[stage], EDGES[stage + 1]))


def kernel(rows_n, cols_n, per_group, slots, table, panel, out, *scratch):
    count = len(PIECES)
    scratch = list(scratch)

    def take(number):
        taken = scratch[:number]
        del scratch[:number]
        return taken

    held = take(STAGES)
    ysend, yrecv, zsend, zrecv = take(count), take(count), take(count), take(count)
    right_hi, right_lo, local_sem, load_recv, load_send, y_send, y_recv, z_send, z_recv = scratch
    row, col = lax.axis_index("row"), lax.axis_index("col")
    chips = rows_n // 2
    far = cols_n // 4
    x, core = row // 2, row % 2
    h, low, y = col // 4, (col // 2) % 2, col % 2
    sibling = (row + 1 - 2 * core, col)
    pair = (row, h * 4 + (1 - low) * 2 + y)
    across = (row, h * 4 + low * 2 + 1 - y)
    beside = [(((x + d) % chips) * 2 + core, col) for d in range(1, chips)]
    ahead = [(row, ((h + d) % far) * 4 + low * 2 + y) for d in range(1, far)]
    partners = [sibling, pair, across] + beside + ahead

    fetches = []
    for stage in range(STAGES):
        fetch = pltpu.make_async_copy(
            panel.at[:, pl.ds(EDGES[stage], EDGES[stage + 1] - EDGES[stage])],
            held[stage].at[pl.ds(row * per_group, per_group), low],
            local_sem.at[stage],
        )
        fetch.start()
        fetches.append(fetch)
    barrier = pltpu.get_barrier_semaphore()
    for device in partners:
        pl.semaphore_signal(barrier, inc=1, device_id=device, device_id_type=MESH)
    pl.semaphore_wait(barrier, len(partners))

    sent = []

    def push(stage, group, side, half, device):
        block = group * per_group + half
        copy = pltpu.make_async_remote_copy(
            src_ref=held[stage].at[block, side],
            dst_ref=held[stage].at[block, side],
            send_sem=load_send.at[len(sent)],
            recv_sem=load_recv.at[stage, block, side],
            device_id=device,
            device_id_type=MESH,
        )
        copy.start()
        sent.append(copy)

    def arrive(stage, group, side, half):
        block = group * per_group + half
        pltpu.make_async_remote_copy(
            src_ref=held[stage].at[block, side],
            dst_ref=held[stage].at[block, side],
            send_sem=load_send.at[0],
            recv_sem=load_recv.at[stage, block, side],
            device_id=sibling,
            device_id_type=MESH,
        ).wait_recv()

    cut = per_group // 2
    ups, downs = list(range(cut)), list(range(cut, per_group))
    others = [((x + chips - d) % chips) * 2 + core for d in range(1, chips)]

    def first(stage):
        fetches[stage].wait()
        for half in ups + downs:
            for device in beside:
                push(stage, row, low, half, device)
        for half in downs + ups:
            push(stage, row, low, half, pair)
        for half in ups + downs:
            push(stage, row, low, half, sibling)

    def second(stage):
        for group in others:
            for half in ups:
                arrive(stage, group, low, half)
                push(stage, group, low, half, pair)
                push(stage, group, low, half, sibling)
        for half in downs:
            arrive(stage, row, 1 - low, half)
            for device in beside:
                push(stage, row, 1 - low, half, device)
            push(stage, row, 1 - low, half, sibling)

    def third(stage):
        for group in others:
            for half in downs:
                arrive(stage, group, low, half)
                push(stage, group, low, half, sibling)
        for half in ups:
            arrive(stage, row, 1 - low, half)
            push(stage, row, 1 - low, half, sibling)
        for group in others:
            for half in ups + downs:
                arrive(stage, group, 1 - low, half)
                push(stage, group, 1 - low, half, sibling)
        for d in range(chips):
            group = ((x + d) % chips) * 2 + 1 - core
            for side in range(2):
                for half in range(per_group):
                    arrive(stage, group, side, half)

    depth = held[0].shape[-1]

    def split(value):
        top = value.astype(jnp.bfloat16)
        return top, (value - top.astype(jnp.float32)).astype(jnp.bfloat16)

    def strips(stage, position, emit, fresh=0):
        left, right = table[0, position], table[1, position]
        for part in range(fresh, stage + 1):
            for side in range(2):
                where = (slice(EDGES[part], EDGES[part + 1]), slice(side * depth, (side + 1) * depth))
                right_hi[where], right_lo[where] = split(held[part][right, side])

        def product(part, begin, end):
            total = None
            for side in range(2):
                span = slice(side * depth, (side + 1) * depth)
                top, rest = split(held[part][left, side])
                for one, two in ((rest, right_hi), (top, right_lo), (top, right_hi)):
                    term = lax.dot_general(one, two[begin:end, span], NT, preferred_element_type=jnp.float32)
                    total = term if total is None else total + term
            return total

        for number, (own_stage, r0, r1, c0, c1) in enumerate(PIECES):
            if own_stage == stage:
                for part in range(STAGES):
                    if r0 <= EDGES[part] < r1:
                        emit(number, EDGES[part] - r0, EDGES[part + 1] - r0, product(part, c0, c1))

    def numbers(stage):
        return [number for number, piece in enumerate(PIECES) if piece[0] == stage]

    def place(d, side_y, slot):
        return (((h + d) % far) * 4 + low * 2 + side_y) * slots + slot

    def y_copy(number, index):
        return pltpu.make_async_remote_copy(
            src_ref=ysend[number].at[index],
            dst_ref=yrecv[number].at[index],
            send_sem=y_send.at[number, index],
            recv_sem=y_recv.at[number, index],
            device_id=across,
            device_id_type=MESH,
        )

    def z_copy(number, index):
        return pltpu.make_async_remote_copy(
            src_ref=zsend[number].at[index],
            dst_ref=zrecv[number].at[index],
            send_sem=z_send.at[number, index],
            recv_sem=z_recv.at[number, index],
            device_id=(row, ((h + index // slots + 1) % far) * 4 + low * 2 + y),
            device_id_type=MESH,
        )

    tiles, hops = far * slots, (far - 1) * slots

    def y_work(stage):
        @pl.loop(0, tiles)
        def _(index):
            def emit(number, begin, end, value):
                ysend[number][index, begin:end, :] = value

            strips(stage, place(index // slots + 1, 1 - y, index % slots), emit)
            for number in numbers(stage):
                y_copy(number, index).start()

    def z_work(stage):
        @pl.loop(0, hops)
        def _(index):
            def emit(number, begin, end, value):
                zsend[number][index, begin:end, :] = value

            strips(stage, place(index // slots + 1, y, index % slots), emit)
            for number in numbers(stage):
                y_copy(number, index).wait_recv()
                zsend[number][index] += yrecv[number][index]
                z_copy(number, index).start()

    first(0)
    for stage in range(STAGES):
        second(stage)
        if stage + 1 < STAGES:
            first(stage + 1)
        if stage:
            z_work(stage - 1)
        third(stage)
        y_work(stage)
    z_work(STAGES - 1)

    @pl.loop(0, slots)
    def _(slot):
        def emit(number, begin, end, value):
            _, r0, _, c0, c1 = PIECES[number]
            out[slot, r0 + begin:r0 + end, c0:c1] = value

        for stage in range(STAGES):
            strips(stage, place(0, y, slot), emit, stage)
        for number, (_, r0, r1, c0, c1) in enumerate(PIECES):
            y_copy(number, hops + slot).wait_recv()
            out[slot, r0:r1, c0:c1] += yrecv[number][hops + slot]

    for number, (_, r0, r1, c0, c1) in enumerate(PIECES):
        @pl.loop(0, hops)
        def _(index):
            z_copy(number, index).wait_recv()
            slot = index % slots
            out[slot, r0:r1, c0:c1] += zrecv[number][index]

    for slot in range(slots):
        live = table[2, place(0, y, slot)]
        out[slot] = jnp.where(live > 0, out[slot], 0.0)

    for copy in sent:
        copy.wait_send()
    for number in range(count):
        @pl.loop(0, tiles)
        def _(index):
            y_copy(number, index).wait_send()

        @pl.loop(0, hops)
        def _(index):
            z_copy(number, index).wait_send()


def body(panel_rows, owner_slot):
    rows_n = lax.axis_size("row")
    cols_n = lax.axis_size("col")
    slab_rows, depth = panel_rows.shape
    per_group = slab_rows // BLOCK
    blocks = per_group * rows_n
    row_tiles = per_group * (blocks - per_group) + per_group * (per_group + 1) // 2
    slots = (row_tiles + cols_n - 1) // cols_n
    positions = cols_n * slots
    table = jnp.stack([part.astype(jnp.int32) for part in slot_table(owner_slot, lax.axis_index("row"), positions, per_group)])
    chips, far = rows_n // 2, cols_n // 4
    pushes = per_group * ((chips - 1) * 4 + 3) + per_group * (chips - 1)
    tiles = far * slots
    hops = (far - 1) * slots
    summed = pl.pallas_call(
        functools.partial(kernel, rows_n, cols_n, per_group, slots),
        out_shape=jax.ShapeDtypeStruct((slots, BLOCK, BLOCK), jnp.float32),
        in_specs=[pl.BlockSpec(memory_space=pltpu.SMEM), pl.BlockSpec(memory_space=pl.ANY)],
        out_specs=pl.BlockSpec(memory_space=pltpu.VMEM),
        scratch_shapes=[pltpu.VMEM((blocks, 2, EDGES[stage + 1] - EDGES[stage], depth), jnp.float32) for stage in range(STAGES)]
        + [
            pltpu.VMEM((number, r1 - r0, c1 - c0), jnp.float32)
            for number in (tiles, tiles, hops, hops)
            for _, r0, r1, c0, c1 in PIECES
        ]
        + [
            pltpu.VMEM((BLOCK, 2 * depth), jnp.bfloat16),
            pltpu.VMEM((BLOCK, 2 * depth), jnp.bfloat16),
            pltpu.SemaphoreType.DMA((STAGES,)),
            pltpu.SemaphoreType.DMA((STAGES, blocks, 2)),
            pltpu.SemaphoreType.DMA((STAGES * pushes,)),
            pltpu.SemaphoreType.DMA((len(PIECES), tiles)),
            pltpu.SemaphoreType.DMA((len(PIECES), tiles)),
            pltpu.SemaphoreType.DMA((len(PIECES), hops)),
            pltpu.SemaphoreType.DMA((len(PIECES), hops)),
        ],
        compiler_params=pltpu.CompilerParams(
            collective_id=0, has_side_effects=True, vmem_limit_bytes=60 * 2**20
        ),
        cost_estimate=pl.CostEstimate(flops=2 * positions * BLOCK * BLOCK * depth, bytes_accessed=2**22, transcendentals=0),
    )(table, panel_rows.reshape(per_group, BLOCK, depth))
    return summed[None]


def solution(mesh):
    placed = (P("row", "col"), P())
    return jax.shard_map(
        body, mesh=mesh, in_specs=placed, out_specs=P("row", "col", None, None), check_vma=False
    )
```

profile of v0, /device:TPU:1, one launch (start us, length us, event | category | flops | bytes accessed | tf_op | source)
XLA Modules:
  0.0 155.8 jit_solution(4358490813730405761)
XLA Ops:
  0.0 0.1 fusion.2
  0.1 0.8 fusion.1
  0.9 0.8 select_reduce_fusion.1
  1.7 0.6 pad_add_fusion.table
  2.3 150.5 %shard_map.28 = f32[2,512,512]{2,1,0:T(8,128)} custom-call(s32[3,16]{1,0:T(4,128)} %pad_add_fusion.table, f32[2,512,512]{2,1,0:T(8,128)} %bitcast.9), custom_call_target="tpu_custom_call" | custom-call | flops 4294967296 | bytes 4194304 | tf_op jit(solution)/shard_map/pallas_call | solution.py:284
  152.8 3.1 %copy.4 = f32[1,2,512,512]{3,2,1,0:T(8,128)} copy(f32[1,2,512,512]{3,2,1,0:T(8,128)} %bitcast.6) | data formatting | bytes 4194304
  (2 shorter events, 0.0 us)
where the time goes:
time: 156 us
  Pallas kernels  150 us (96%)
  local copies, waits for them, and re-layouts  3.08 us (2%)
  other arithmetic  2.25 us (1%)
    pallas_call x1, Pallas kernels, body(): pl.pallas_call(functools.partial(kernel, rows_n, cols_n, per_group, slots...  150 us

commit v1 on v0

--- a/solution.py
+++ b/solution.py
@@ -267,7 +267,7 @@
             z_copy(number, index).wait_send()
 
 
-def body(panel_rows, owner_slot):
+def general(panel_rows, owner_slot):
     rows_n = lax.axis_size("row")
     cols_n = lax.axis_size("col")
     slab_rows, depth = panel_rows.shape
@@ -311,6 +311,339 @@
     return summed[None]
 
 
+STRIPS = 8
+WIDE = 4
+FAR, ACROSS, PASS, OWN = range(4)
+
+
+def fast_pieces():
+    width, lanes = BLOCK // STRIPS, BLOCK // WIDE
+    pieces = []
+    for stage in range(STRIPS):
+        reach = min(lanes * (stage + 1), BLOCK)
+        pieces.append((stage, width * stage, width * (stage + 1), 0, reach))
+        if 0 < stage < WIDE:
+            pieces.append((stage, 0, width * stage, reach - lanes, reach))
+    return pieces
+
+
+FAST_PIECES = fast_pieces()
+
+
+def fast_kernel(slots, owner, panel, out, *scratch):
+    count = len(FAST_PIECES)
+    scratch = list(scratch)
+
+    def take(number):
+        taken = scratch[:number]
+        del scratch[:number]
+        return taken
+
+    ysend, yrecv, zsend, zrecv = take(count), take(count), take(count), take(count)
+    held, high, rest, total, table, local_sem, load_recv, load_send, y_send, y_recv, z_send, z_recv = scratch
+    per_group = panel.shape[0]
+    depth = panel.shape[-1]
+    width, lanes = BLOCK // STRIPS, BLOCK // WIDE
+    row, col = lax.axis_index("row"), lax.axis_index("col")
+    x, core = row // 2, row % 2
+    h, low, y = col // 4, (col // 2) % 2, col % 2
+    sibling = (row + 1 - 2 * core, col)
+    pair = (row, h * 4 + (1 - low) * 2 + y)
+    across = (row, h * 4 + low * 2 + 1 - y)
+    opposite = (row, (1 - h) * 4 + (1 - low) * 2 + y)
+    beside = ((1 - x) * 2 + core, col)
+    partners = [sibling, pair, across, opposite, beside]
+    halves = range(per_group)
+
+    fetches = []
+    for strip in range(STRIPS):
+        fetch = pltpu.make_async_copy(
+            panel.at[:, pl.ds(strip * width, width)],
+            held.at[pl.ds(row * per_group, per_group), low, pl.ds(strip * width, width)],
+            local_sem.at[strip],
+        )
+        fetch.start()
+        fetches.append(fetch)
+    barrier = pltpu.get_barrier_semaphore()
+    for device in partners:
+        pl.semaphore_signal(barrier, inc=1, device_id=device, device_id_type=MESH)
+    pl.semaphore_wait(barrier, len(partners))
+
+    always, first_x, second_x = [], [], []
+
+    def load_copy(number, strip, group, half, side, device):
+        block = group * per_group + half
+        where = held.at[block, side, pl.ds(strip * width, width)]
+        return pltpu.make_async_remote_copy(
+            src_ref=where,
+            dst_ref=where,
+            send_sem=load_send.at[number],
+            recv_sem=load_recv.at[strip, block, side],
+            device_id=device,
+            device_id_type=MESH,
+        )
+
+    def push(strip, group, half, side, device, log):
+        entry = (len(always) + len(first_x) + len(second_x), strip, group, half, side, device)
+        load_copy(*entry).start()
+        log.append(entry)
+
+    def arrive(strip, group, half, side):
+        load_copy(0, strip, group, half, side, sibling).wait_recv()
+
+    def ahead(strip):
+        @pl.when(x == 0)
+        def _():
+            for half in halves:
+                push(strip, row, half, low, beside, first_x)
+
+    def begin(strip):
+        fetches[strip].wait()
+        if strip == 0:
+            ahead(0)
+        for half in halves:
+            push(strip, row, half, low, pair, always)
+        for half in halves:
+            push(strip, row, half, low, sibling, always)
+
+    other, flip = x * 2 + 1 - core, 1 - low
+
+    def gather(stage):
+        strips = (2 * stage, 2 * stage + 1) if stage < WIDE else ()
+        for strip in strips:
+            for half in halves:
+                arrive(strip, row, half, flip)
+
+                @pl.when(x == 0)
+                def _():
+                    push(strip, row, half, flip, beside, first_x)
+
+                push(strip, row, half, flip, sibling, always)
+            if strip + 1 < STRIPS:
+                ahead(strip + 1)
+
+        @pl.when(x == 1)
+        def _():
+            for side in (low, flip):
+                for half in halves:
+                    arrive(stage, core, half, side)
+                    push(stage, core, half, side, sibling, second_x)
+
+        for strip in strips:
+            for side in range(2):
+                for half in halves:
+                    arrive(strip, other, half, side)
+
+        @pl.when(x == 1)
+        def _():
+            for side in range(2):
+                for half in halves:
+                    arrive(stage, 1 - core, half, side)
+
+    def split(block, begin_row, rows):
+        for side in range(2):
+            value = held[block, side, begin_row:begin_row + rows, :]
+            top = value.astype(jnp.bfloat16)
+            span = slice(side * depth, (side + 1) * depth)
+            high[block, begin_row:begin_row + rows, span] = top
+            rest[block, begin_row:begin_row + rows, span] = (value - top.astype(jnp.float32)).astype(jnp.bfloat16)
+
+    def convert(stage):
+        @pl.loop(0, per_group)
+        def _(half):
+            if stage < WIDE:
+                split(row * per_group + half, lanes * stage, lanes)
+            split(other * per_group + half, width * stage, width)
+
+        @pl.when(x == 1)
+        def _():
+            @pl.loop(0, 2 * per_group)
+            def _(block):
+                split(block, width * stage, width)
+
+    for kind, place in (
+        (FAR, (1 - h) * 4 + (1 - low) * 2 + 1 - y),
+        (ACROSS, h * 4 + low * 2 + 1 - y),
+        (PASS, (1 - h) * 4 + (1 - low) * 2 + y),
+        (OWN, h * 4 + low * 2 + y),
+    ):
+        for slot in range(slots):
+            position = place * slots + slot
+            left, right, live = row * per_group, row * per_group, 0
+            for half in halves:
+                for block in range(owner.shape[1]):
+                    hit = owner[row * per_group + half, block] == position
+                    left = jnp.where(hit, row * per_group + half, left)
+                    right = jnp.where(hit, block, right)
+                    live = jnp.where(hit, 1, live)
+            table[0, kind * slots + slot] = left
+            table[1, kind * slots + slot] = right
+            table[2, kind * slots + slot] = live
+
+    def numbers(stage):
+        return [number for number, piece in enumerate(FAST_PIECES) if piece[0] == stage]
+
+    def product(number, entry):
+        _, r0, r1, c0, c1 = FAST_PIECES[number]
+        wide, tall = table[0, entry], table[1, entry]
+        top, low_part = high[tall, r0:r1, :], rest[tall, r0:r1, :]
+        both = lax.dot_general(
+            jnp.concatenate([top, low_part], axis=0), high[wide, c0:c1, :], NT, preferred_element_type=jnp.float32
+        )
+        cross = lax.dot_general(top, rest[wide, c0:c1, :], NT, preferred_element_type=jnp.float32)
+        return both[r1 - r0:] + cross + both[:r1 - r0]
+
+    def y_copy(number, index):
+        return pltpu.make_async_remote_copy(
+            src_ref=ysend[number].at[index],
+            dst_ref=yrecv[number].at[index],
+            send_sem=y_send.at[number, index],
+            recv_sem=y_recv.at[number, index],
+            device_id=across,
+            device_id_type=MESH,
+        )
+
+    def z_copy(number, index):
+        return pltpu.make_async_remote_copy(
+            src_ref=zsend[number].at[index],
+            dst_ref=zrecv[number].at[index],
+            send_sem=z_send.at[number, index],
+            recv_sem=z_recv.at[number, index],
+            device_id=opposite,
+            device_id_type=MESH,
+        )
+
+    def y_work(stage, kind):
+        @pl.loop(0, slots)
+        def _(slot):
+            index = kind * slots + slot
+            for number in numbers(stage):
+                ysend[number][index] = product(number, index)
+                y_copy(number, index).start()
+
+    def z_work(stage):
+        @pl.loop(0, slots)
+        def _(slot):
+            for number in numbers(stage):
+                value = product(number, PASS * slots + slot)
+                y_copy(number, FAR * slots + slot).wait_recv()
+                zsend[number][slot] = value + yrecv[number][FAR * slots + slot]
+                z_copy(number, slot).start()
+
+    def own_work(stage):
+        @pl.loop(0, slots)
+        def _(slot):
+            for number in numbers(stage):
+                _, r0, r1, c0, c1 = FAST_PIECES[number]
+                total[slot, r0:r1, c0:c1] = product(number, OWN * slots + slot)
+
+    def collect(stage):
+        for number in numbers(stage):
+            _, r0, r1, c0, c1 = FAST_PIECES[number]
+
+            @pl.loop(0, slots)
+            def _(slot):
+                y_copy(number, ACROSS * slots + slot).wait_recv()
+                z_copy(number, slot).wait_recv()
+                total[slot, r0:r1, c0:c1] += yrecv[number][ACROSS * slots + slot] + zrecv[number][slot]
+
+    def finish(part):
+        for slot in range(slots):
+            live = table[2, OWN * slots + slot]
+            for c0 in range(0, BLOCK, lanes):
+                value = total[slot, part * lanes:(part + 1) * lanes, c0:c0 + lanes].T
+                out[slot, c0:c0 + lanes, part * lanes:(part + 1) * lanes] = jnp.where(live > 0, value, 0.0)
+
+    for strip in range(4):
+        begin(strip)
+    for stage in range(STRIPS):
+        gather(stage)
+        for strip in (2 * stage + 4, 2 * stage + 5):
+            if strip < STRIPS:
+                begin(strip)
+        convert(stage)
+        y_work(stage, FAR)
+        y_work(stage, ACROSS)
+        own_work(stage)
+        z_work(stage)
+    for stage in range(STRIPS):
+        collect(stage)
+        if stage >= WIDE - 1 and stage % 2:
+            for part in ((0, 1) if stage == WIDE - 1 else (stage // 2,)):
+                finish(part)
+
+    for entry in always:
+        load_copy(*entry).wait_send()
+
+    @pl.when(x == 0)
+    def _():
+        for entry in first_x:
+            load_copy(*entry).wait_send()
+
+    @pl.when(x == 1)
+    def _():
+        for entry in second_x:
+            load_copy(*entry).wait_send()
+
+    for number in range(count):
+        @pl.loop(0, 2 * slots)
+        def _(index):
+            y_copy(number, index).wait_send()
+
+        @pl.loop(0, slots)
+        def _(index):
+            z_copy(number, index).wait_send()
+
+
+def quick(panel_rows, owner_slot):
+    rows_n = lax.axis_size("row")
+    cols_n = lax.axis_size("col")
+    slab_rows, depth = panel_rows.shape
+    per_group = slab_rows // BLOCK
+    blocks = per_group * rows_n
+    row_tiles = per_group * (blocks - per_group) + per_group * (per_group + 1) // 2
+    slots = (row_tiles + cols_n - 1) // cols_n
+    positions = cols_n * slots
+    count = len(FAST_PIECES)
+    pushes = STRIPS * per_group * 7
+    summed = pl.pallas_call(
+        functools.partial(fast_kernel, slots),
+        out_shape=jax.ShapeDtypeStruct((slots, BLOCK, BLOCK), jnp.float32),
+        in_specs=[pl.BlockSpec(memory_space=pltpu.SMEM), pl.BlockSpec(memory_space=pl.ANY)],
+        out_specs=pl.BlockSpec(memory_space=pltpu.VMEM),
+        scratch_shapes=[
+            pltpu.VMEM((number, r1 - r0, c1 - c0), jnp.float32)
+            for number in (2 * slots, 2 * slots, slots, slots)
+            for _, r0, r1, c0, c1 in FAST_PIECES
+        ]
+        + [
+            pltpu.VMEM((blocks, 2, BLOCK, depth), jnp.float32),
+            pltpu.VMEM((blocks, BLOCK, 2 * depth), jnp.bfloat16),
+            pltpu.VMEM((blocks, BLOCK, 2 * depth), jnp.bfloat16),
+            pltpu.VMEM((slots, BLOCK, BLOCK), jnp.float32),
+            pltpu.SMEM((3, 4 * slots), jnp.int32),
+            pltpu.SemaphoreType.DMA((STRIPS,)),
+            pltpu.SemaphoreType.DMA((STRIPS, blocks, 2)),
+            pltpu.SemaphoreType.DMA((pushes,)),
+            pltpu.SemaphoreType.DMA((count, 2 * slots)),
+            pltpu.SemaphoreType.DMA((count, 2 * slots)),
+            pltpu.SemaphoreType.DMA((count, slots)),
+            pltpu.SemaphoreType.DMA((count, slots)),
+        ],
+        compiler_params=pltpu.CompilerParams(
+            collective_id=0, has_side_effects=True, vmem_limit_bytes=60 * 2**20
+        ),
+        cost_estimate=pl.CostEstimate(flops=2 * positions * BLOCK * BLOCK * depth, bytes_accessed=2**22, transcendentals=0),
+    )(owner_slot, panel_rows.reshape(per_group, BLOCK, depth))
+    return summed[None]
+
+
+def body(panel_rows, owner_slot):
+    if lax.axis_size("row") == 4 and lax.axis_size("col") == 8:
+        return quick(panel_rows, owner_slot)
+    return general(panel_rows, owner_slot)
+
+
 def solution(mesh):
     placed = (P("row", "col"), P())
     return jax.shard_map(

time: 156 us -> 142 us (0.910)
  the two profiles are of different devices: /device:TPU:1 before, /device:TPU:19 now
where the time goes in v1:
time: 142 us
  Pallas kernels  139 us (98%)
  local copies, waits for them, and re-layouts  3.08 us (2%)
    pallas_call x1, Pallas kernels, quick(): pl.pallas_call(functools.partial(fast_kernel, slots), out_shape=jax.Shape...  139 us
    unnamed x1, local copies, waits for them, and re-layouts  3.08 us

profile of v1, /device:TPU:19, one launch (start us, length us, event | category | flops | bytes accessed | tf_op | source)
XLA Modules:
  0.0 141.7 jit_solution(1487339992456460256)
XLA Ops:
  0.0 138.6 %shard_map.28 = f32[2,512,512]{2,1,0:T(8,128)} custom-call(s32[8,8]{1,0:T(8,128)} %owner.1, f32[2,512,512]{2,1,0:T(8,128)} %bitcast.3), custom_call_target="tpu_custom_call" | custom-call | flops 4294967296 | bytes 4194304 | tf_op jit(solution)/shard_map/pallas_call | solution.py:609
  138.6 3.1 %copy.4 = f32[1,2,512,512]{3,2,1,0:T(8,128)} copy(f32[1,2,512,512]{3,2,1,0:T(8,128)} %bitcast.2) | data formatting | bytes 4194304

commit v2 on v0

--- a/solution.py
+++ b/solution.py
@@ -267,7 +267,7 @@
             z_copy(number, index).wait_send()
 
 
-def body(panel_rows, owner_slot):
+def general(panel_rows, owner_slot):
     rows_n = lax.axis_size("row")
     cols_n = lax.axis_size("col")
     slab_rows, depth = panel_rows.shape
@@ -311,6 +311,360 @@
     return summed[None]
 
 
+LANES = 128
+TALL = (0, 64, 128, 192, 256, 320, 384, 448, 512)
+REACH = (128, 256, 384, 512, 512, 512, 512, 512)
+STEP = 64
+STEPS = BLOCK // STEP
+AREAS = ((3, 0, 128), (3, 128, 256), (5, 256, 384), (7, 384, 512))
+FULL = REACH.index(BLOCK)
+FAST_STAGES = len(REACH)
+FIRST = 4
+PLAN = ((0, 0), (1, 0), (2, 0), (4, 4), (4, 5), (0, 1), (1, 1), (2, 1), (4, 6), (4, 7), (0, 2), (1, 2), (2, 2), (0, 3), (1, 3), (2, 3), (0, 4), (0, 5), (2, 4), (1, 4), (3, 3), (0, 6), (2, 5), (1, 5), (3, 5), (0, 7), (2, 6), (1, 6), (1, 7), (2, 7), (3, 7))
+HELD = ()
+FAR, ACROSS, PASS, OWN = range(4)
+
+
+def fast_pieces():
+    pieces, before = [], 0
+    for stage, reach in enumerate(REACH):
+        pieces.append((stage, TALL[stage], TALL[stage + 1], 0, reach))
+        if stage and reach > before:
+            pieces.append((stage, 0, TALL[stage], before, reach))
+        before = reach
+    return pieces
+
+
+FAST_PIECES = fast_pieces()
+
+
+def fast_kernel(slots, owner, panel, out, *scratch):
+    count = len(FAST_PIECES)
+    scratch = list(scratch)
+
+    def take(number):
+        taken = scratch[:number]
+        del scratch[:number]
+        return taken
+
+    ysend, yrecv, zsend, zrecv = take(count), take(count), take(count), take(count)
+    held, high, rest, total, done, table, local_sem, load_recv, cross_recv, load_send, y_send, f_recv, o_recv, z_send, z_recv, out_sem = scratch
+    per_group = panel.shape[0]
+    depth = panel.shape[-1]
+    row, col = lax.axis_index("row"), lax.axis_index("col")
+    x, core = row // 2, row % 2
+    h, low, y = col // 4, (col // 2) % 2, col % 2
+    sibling = (row + 1 - 2 * core, col)
+    pair = (row, h * 4 + (1 - low) * 2 + y)
+    across = (row, h * 4 + low * 2 + 1 - y)
+    opposite = (row, (1 - h) * 4 + (1 - low) * 2 + y)
+    beside = ((1 - x) * 2 + core, col)
+    partners = [sibling, pair, across, opposite, beside]
+    halves = range(per_group)
+
+    fetches = []
+    for step in range(STEPS):
+        fetch = pltpu.make_async_copy(
+            panel.at[:, pl.ds(step * STEP, STEP)],
+            held.at[pl.ds(row * per_group, per_group), low, pl.ds(step * STEP, STEP)],
+            local_sem.at[step],
+        )
+        fetch.start()
+        fetches.append(fetch)
+    barrier = pltpu.get_barrier_semaphore()
+    for device in partners:
+        pl.semaphore_signal(barrier, inc=1, device_id=device, device_id_type=MESH)
+    pl.semaphore_wait(barrier, len(partners))
+
+    def load_copy(arrivals, step, group, side, device, kind):
+        rows = pl.ds(0, BLOCK) if step is None else pl.ds(step * STEP, STEP)
+        where = held.at[pl.ds(group * per_group, per_group), side, rows]
+        return pltpu.make_async_remote_copy(
+            src_ref=where,
+            dst_ref=where,
+            send_sem=load_send.at[kind],
+            recv_sem=arrivals.at[0 if step is None else step, group % 2, side],
+            device_id=device,
+            device_id_type=MESH,
+        )
+
+    def push(arrivals, step, group, side, device, kind):
+        load_copy(arrivals, step, group, side, device, kind).start()
+
+    def arrive(arrivals, step, group, side):
+        load_copy(arrivals, step, group, side, sibling, 0).wait_recv()
+
+    other, flip = x * 2 + 1 - core, 1 - low
+
+    def forward(step, side, kind):
+        @pl.when(x == 0)
+        def _():
+            push(cross_recv, step, row, side, beside, kind)
+
+    def begin(step):
+        fetches[step].wait()
+        if step == 0:
+            forward(0, low, 3)
+        push(load_recv, step, row, low, pair, 0)
+        push(load_recv, step, row, low, sibling, 1)
+
+    def gather(stage):
+        start = REACH[stage - 1] if stage else 0
+        steps = range(start // STEP, REACH[stage] // STEP)
+        parts = range(TALL[stage] // STEP, TALL[stage + 1] // STEP)
+        for step in steps:
+            arrive(load_recv, step, row, flip)
+            forward(step, flip, 4)
+            if step + 1 < STEPS:
+                forward(step + 1, low, 3)
+            push(load_recv, step, row, flip, sibling, 2)
+
+        @pl.when(x == 1)
+        def _():
+            for part in parts:
+                for kind, side in ((5, low), (6, flip)):
+                    arrive(cross_recv, part, core, side)
+                    push(cross_recv, part, core, side, sibling, kind)
+
+        for step in steps:
+            for side in range(2):
+                arrive(load_recv, step, other, side)
+
+        @pl.when(x == 1)
+        def _():
+            for part in parts:
+                for side in range(2):
+                    arrive(cross_recv, part, 1 - core, side)
+
+    def split(block, begin_row, end_row):
+        for side in range(2):
+            value = held[block, side, begin_row:end_row, :]
+            top = value.astype(jnp.bfloat16)
+            span = slice(side * depth, (side + 1) * depth)
+            high[block, begin_row:end_row, span] = top
+            rest[block, begin_row:end_row, span] = (value - top.astype(jnp.float32)).astype(jnp.bfloat16)
+
+    def convert(stage):
+        start = REACH[stage - 1] if stage else 0
+
+        @pl.loop(0, per_group)
+        def _(half):
+            if start < REACH[stage]:
+                split(row * per_group + half, start, REACH[stage])
+            split(other * per_group + half, TALL[stage], TALL[stage + 1])
+
+        @pl.when(x == 1)
+        def _():
+            @pl.loop(0, 2 * per_group)
+            def _(block):
+                split(block, TALL[stage], TALL[stage + 1])
+
+    def numbers(stage):
+        return [number for number, piece in enumerate(FAST_PIECES) if piece[0] == stage]
+
+    def product(area, entry):
+        r0, r1, c0, c1 = area
+        wide, tall = table[0, entry], table[1, entry]
+        top, low_part = high[tall, r0:r1, :], rest[tall, r0:r1, :]
+        both = lax.dot_general(
+            jnp.concatenate([top, low_part], axis=0), high[wide, c0:c1, :], NT, preferred_element_type=jnp.float32
+        )
+        cross = lax.dot_general(top, rest[wide, c0:c1, :], NT, preferred_element_type=jnp.float32)
+        return both[r1 - r0:] + cross + both[:r1 - r0]
+
+    def y_copy(number, kind, index):
+        return pltpu.make_async_remote_copy(
+            src_ref=ysend[number].at[index],
+            dst_ref=yrecv[number].at[index],
+            send_sem=y_send,
+            recv_sem=(f_recv.at[number, index] if kind == FAR else o_recv.at[number]),
+            device_id=across,
+            device_id_type=MESH,
+        )
+
+    def z_copy(number, index):
+        return pltpu.make_async_remote_copy(
+            src_ref=zsend[number].at[index],
+            dst_ref=zrecv[number].at[index],
+            send_sem=z_send,
+            recv_sem=z_recv.at[number],
+            device_id=opposite,
+            device_id_type=MESH,
+        )
+
+    def y_work(stage, kind):
+        @pl.loop(0, slots)
+        def _(slot):
+            index = kind * slots + slot
+            for number in numbers(stage):
+                ysend[number][index] = product(FAST_PIECES[number][1:], index)
+                y_copy(number, kind, index).start()
+
+    def z_work(stage):
+        @pl.loop(0, slots)
+        def _(slot):
+            for number in numbers(stage):
+                value = product(FAST_PIECES[number][1:], PASS * slots + slot)
+                y_copy(number, FAR, FAR * slots + slot).wait_recv()
+                zsend[number][slot] = value + yrecv[number][FAR * slots + slot]
+                if stage in HELD:
+                    @pl.when(h != low)
+                    def _():
+                        z_copy(number, slot).start()
+                else:
+                    z_copy(number, slot).start()
+
+    def release(stage):
+        @pl.when(h == low)
+        def _():
+            for number in numbers(stage):
+                @pl.loop(0, slots)
+                def _(slot):
+                    z_copy(number, slot).start()
+
+    def own_work(stage):
+        @pl.loop(0, slots)
+        def _(slot):
+            for last, r0, r1 in AREAS:
+                if last == stage:
+                    total[slot, r0:r1, :] = product((r0, r1, 0, BLOCK), OWN * slots + slot)
+
+    def collect(stage):
+        for number in numbers(stage):
+            _, r0, r1, c0, c1 = FAST_PIECES[number]
+            y_copy(number, ACROSS, pl.ds(ACROSS * slots, slots)).wait_recv()
+            z_copy(number, pl.ds(0, slots)).wait_recv()
+
+            @pl.loop(0, slots)
+            def _(slot):
+                total[slot, r0:r1, c0:c1] += yrecv[number][ACROSS * slots + slot] + zrecv[number][slot]
+
+    def store(part, slot):
+        span = pl.ds(part * LANES, LANES)
+        return pltpu.make_async_copy(done.at[slot, :, span], out.at[slot, :, span], out_sem.at[part, slot])
+
+    def finish(part):
+        for slot in range(slots):
+            live = table[2, OWN * slots + slot]
+            for c0 in range(0, BLOCK, LANES):
+                value = total[slot, part * LANES:(part + 1) * LANES, c0:c0 + LANES].T
+                done[slot, c0:c0 + LANES, part * LANES:(part + 1) * LANES] = jnp.where(live > 0, value, 0.0)
+            store(part, slot).start()
+
+    for step in range(FIRST):
+        begin(step)
+    for kind, place in (
+        (FAR, (1 - h) * 4 + (1 - low) * 2 + 1 - y),
+        (ACROSS, h * 4 + low * 2 + 1 - y),
+        (PASS, (1 - h) * 4 + (1 - low) * 2 + y),
+        (OWN, h * 4 + low * 2 + y),
+    ):
+        for slot in range(slots):
+            position = place * slots + slot
+            left, right, live = row * per_group, row * per_group, 0
+            for half in halves:
+                for block in range(owner.shape[1]):
+                    hit = owner[row * per_group + half, block] == position
+                    left = jnp.where(hit, row * per_group + half, left)
+                    right = jnp.where(hit, block, right)
+                    live = jnp.where(hit, 1, live)
+            table[0, kind * slots + slot] = left
+            table[1, kind * slots + slot] = right
+            table[2, kind * slots + slot] = live
+
+    def supply(stage):
+        gather(stage)
+        convert(stage)
+        y_work(stage, FAR)
+
+    def relay(stage):
+        y_work(stage, ACROSS)
+
+    acts = (supply, relay, z_work, own_work, begin, release)
+    for act, argument in PLAN:
+        acts[act](argument)
+    ready = 0
+    for stage in range(FAST_STAGES):
+        collect(stage)
+        while stage >= FULL and (ready + 1) * LANES <= TALL[stage + 1]:
+            finish(ready)
+            ready += 1
+
+    for side, kind in ((low, 0), (low, 1), (flip, 2)):
+        load_copy(load_recv, None, row, side, sibling, kind).wait_send()
+
+    @pl.when(x == 0)
+    def _():
+        for side, kind in ((low, 3), (flip, 4)):
+            load_copy(cross_recv, None, row, side, sibling, kind).wait_send()
+
+    @pl.when(x == 1)
+    def _():
+        for side, kind in ((low, 5), (flip, 6)):
+            load_copy(cross_recv, None, core, side, sibling, kind).wait_send()
+
+    for area, sem in ((held.at[pl.ds(0, slots)], y_send), (held.at[pl.ds(0, slots), 0], z_send)):
+        pltpu.make_async_remote_copy(
+            src_ref=area, dst_ref=area, send_sem=sem, recv_sem=o_recv.at[0], device_id=across, device_id_type=MESH
+        ).wait_send()
+
+    for part in range(BLOCK // LANES):
+        for slot in range(slots):
+            store(part, slot).wait()
+
+
+def quick(panel_rows, owner_slot):
+    rows_n = lax.axis_size("row")
+    cols_n = lax.axis_size("col")
+    slab_rows, depth = panel_rows.shape
+    per_group = slab_rows // BLOCK
+    blocks = per_group * rows_n
+    row_tiles = per_group * (blocks - per_group) + per_group * (per_group + 1) // 2
+    slots = (row_tiles + cols_n - 1) // cols_n
+    positions = cols_n * slots
+    count = len(FAST_PIECES)
+    summed = pl.pallas_call(
+        functools.partial(fast_kernel, slots),
+        out_shape=jax.ShapeDtypeStruct((slots, BLOCK, BLOCK), jnp.float32),
+        in_specs=[pl.BlockSpec(memory_space=pltpu.SMEM), pl.BlockSpec(memory_space=pl.ANY)],
+        out_specs=pl.BlockSpec(memory_space=pl.ANY),
+        scratch_shapes=[
+            pltpu.VMEM((number, r1 - r0, c1 - c0), jnp.float32)
+            for number in (2 * slots, 2 * slots, slots, slots)
+            for _, r0, r1, c0, c1 in FAST_PIECES
+        ]
+        + [
+            pltpu.VMEM((blocks, 2, BLOCK, depth), jnp.float32),
+            pltpu.VMEM((blocks, BLOCK, 2 * depth), jnp.bfloat16),
+            pltpu.VMEM((blocks, BLOCK, 2 * depth), jnp.bfloat16),
+            pltpu.VMEM((slots, BLOCK, BLOCK), jnp.float32),
+            pltpu.VMEM((slots, BLOCK, BLOCK), jnp.float32),
+            pltpu.SMEM((3, 4 * slots), jnp.int32),
+            pltpu.SemaphoreType.DMA((STEPS,)),
+            pltpu.SemaphoreType.DMA((STEPS, 2, 2)),
+            pltpu.SemaphoreType.DMA((STEPS, 2, 2)),
+            pltpu.SemaphoreType.DMA((7,)),
+            pltpu.SemaphoreType.DMA(()),
+            pltpu.SemaphoreType.DMA((count, slots)),
+            pltpu.SemaphoreType.DMA((count,)),
+            pltpu.SemaphoreType.DMA(()),
+            pltpu.SemaphoreType.DMA((count,)),
+            pltpu.SemaphoreType.DMA((BLOCK // LANES, slots)),
+        ],
+        compiler_params=pltpu.CompilerParams(
+            collective_id=0, has_side_effects=True, vmem_limit_bytes=60 * 2**20
+        ),
+        cost_estimate=pl.CostEstimate(flops=2 * positions * BLOCK * BLOCK * depth, bytes_accessed=2**22, transcendentals=0),
+    )(owner_slot, panel_rows.reshape(per_group, BLOCK, depth))
+    return summed[None]
+
+
+def body(panel_rows, owner_slot):
+    if lax.axis_size("row") == 4 and lax.axis_size("col") == 8:
+        return quick(panel_rows, owner_slot)
+    return general(panel_rows, owner_slot)
+
+
 def solution(mesh):
     placed = (P("row", "col"), P())
     return jax.shard_map(

time: 156 us -> 136 us (0.87)
  the two profiles are of different devices: /device:TPU:1 before, /device:TPU:19 now
where the time goes in v2:
time: 136 us; the launch traced here: 135 us
  Pallas kernels  132 us (97%)
  local copies, waits for them, and re-layouts  3.08 us (2%)
    pallas_call x1, Pallas kernels, quick(): pl.pallas_call(functools.partial(fast_kernel, slots), out_shape=jax.Shape...  132 us
    unnamed x1, local copies, waits for them, and re-layouts  3.08 us

profile of v2, /device:TPU:19, one launch (start us, length us, event | category | flops | bytes accessed | tf_op | source)
XLA Modules:
  0.0 135.3 jit_solution(10795240759008140420)
XLA Ops:
  0.0 132.3 %shard_map.28 = f32[2,512,512]{2,1,0:T(8,128)} custom-call(s32[8,8]{1,0:T(8,128)} %owner.1, f32[2,512,512]{2,1,0:T(8,128)} %bitcast.3), custom_call_target="tpu_custom_call" | custom-call | flops 4294967296 | bytes 4194304 | tf_op jit(solution)/shard_map/pallas_call | solution.py:626
  132.3 3.1 %copy.4 = f32[1,2,512,512]{3,2,1,0:T(8,128)} copy(f32[1,2,512,512]{3,2,1,0:T(8,128)} %bitcast.2) | data formatting | bytes 4194304

commit v3 on v2

--- a/solution.py
+++ b/solution.py
@@ -348,7 +348,7 @@
         return taken
 
     ysend, yrecv, zsend, zrecv = take(count), take(count), take(count), take(count)
-    held, high, rest, total, done, table, local_sem, load_recv, cross_recv, load_send, y_send, f_recv, o_recv, z_send, z_recv, out_sem = scratch
+    held, high, rest, total, table, local_sem, load_recv, cross_recv, load_send, y_send, f_recv, o_recv, z_send, z_recv = scratch
     per_group = panel.shape[0]
     depth = panel.shape[-1]
     row, col = lax.axis_index("row"), lax.axis_index("col")
@@ -539,17 +539,12 @@
             def _(slot):
                 total[slot, r0:r1, c0:c1] += yrecv[number][ACROSS * slots + slot] + zrecv[number][slot]
 
-    def store(part, slot):
-        span = pl.ds(part * LANES, LANES)
-        return pltpu.make_async_copy(done.at[slot, :, span], out.at[slot, :, span], out_sem.at[part, slot])
-
     def finish(part):
         for slot in range(slots):
             live = table[2, OWN * slots + slot]
             for c0 in range(0, BLOCK, LANES):
                 value = total[slot, part * LANES:(part + 1) * LANES, c0:c0 + LANES].T
-                done[slot, c0:c0 + LANES, part * LANES:(part + 1) * LANES] = jnp.where(live > 0, value, 0.0)
-            store(part, slot).start()
+                out[slot, c0:c0 + LANES, part * LANES:(part + 1) * LANES] = jnp.where(live > 0, value, 0.0)
 
     for step in range(FIRST):
         begin(step)
@@ -608,10 +603,6 @@
             src_ref=area, dst_ref=area, send_sem=sem, recv_sem=o_recv.at[0], device_id=across, device_id_type=MESH
         ).wait_send()
 
-    for part in range(BLOCK // LANES):
-        for slot in range(slots):
-            store(part, slot).wait()
-
 
 def quick(panel_rows, owner_slot):
     rows_n = lax.axis_size("row")
@@ -625,9 +616,9 @@
     count = len(FAST_PIECES)
     summed = pl.pallas_call(
         functools.partial(fast_kernel, slots),
-        out_shape=jax.ShapeDtypeStruct((slots, BLOCK, BLOCK), jnp.float32),
+        out_shape=pltpu.VMEM((slots, BLOCK, BLOCK), jnp.float32),
         in_specs=[pl.BlockSpec(memory_space=pltpu.SMEM), pl.BlockSpec(memory_space=pl.ANY)],
-        out_specs=pl.BlockSpec(memory_space=pl.ANY),
+        out_specs=pl.BlockSpec(memory_space=pltpu.VMEM),
         scratch_shapes=[
             pltpu.VMEM((number, r1 - r0, c1 - c0), jnp.float32)
             for number in (2 * slots, 2 * slots, slots, slots)
@@ -637,7 +628,6 @@
             pltpu.VMEM((blocks, 2, BLOCK, depth), jnp.float32),
             pltpu.VMEM((blocks, BLOCK, 2 * depth), jnp.bfloat16),
             pltpu.VMEM((blocks, BLOCK, 2 * depth), jnp.bfloat16),
-            pltpu.VMEM((slots, BLOCK, BLOCK), jnp.float32),
             pltpu.VMEM((slots, BLOCK, BLOCK), jnp.float32),
             pltpu.SMEM((3, 4 * slots), jnp.int32),
             pltpu.SemaphoreType.DMA((STEPS,)),
@@ -649,10 +639,9 @@
             pltpu.SemaphoreType.DMA((count,)),
             pltpu.SemaphoreType.DMA(()),
             pltpu.SemaphoreType.DMA((count,)),
-            pltpu.SemaphoreType.DMA((BLOCK // LANES, slots)),
         ],
         compiler_params=pltpu.CompilerParams(
-            collective_id=0, has_side_effects=True, vmem_limit_bytes=60 * 2**20
+            collective_id=0, has_side_effects=True, vmem_limit_bytes=54 * 2**20
         ),
         cost_estimate=pl.CostEstimate(flops=2 * positions * BLOCK * BLOCK * depth, bytes_accessed=2**22, transcendentals=0),
     )(owner_slot, panel_rows.reshape(per_group, BLOCK, depth))

time: 136 us -> 133 us (0.978)
  local copies, waits for them, and re-layouts: 3.08 us -> 1.32 us
    unnamed x1, local copies, waits for them, and re-layouts: 3.08 us -> 1.32 us
where the time goes in v3:
time: 133 us
  Pallas kernels  131 us (98%)
    pallas_call x1, Pallas kernels, quick(): pl.pallas_call(functools.partial(fast_kernel, slots), out_shape=pltpu.VME...  131 us

profile of v3, /device:TPU:19, one launch (start us, length us, event | category | flops | bytes accessed | tf_op | source)
XLA Modules:
  0.0 132.7 jit_solution(1511269893692178908)
XLA Ops:
  0.0 131.4 %shard_map.28 = f32[2,512,512]{2,1,0:T(8,128)S(1)} custom-call(s32[8,8]{1,0:T(8,128)} %owner.1, f32[2,512,512]{2,1,0:T(8,128)} %bitcast.3), custom_call_target="tpu_custom_call" | custom-call | flops 4294967296 | bytes 4194304 | tf_op jit(solution)/shard_map/pallas_call | solution.py:617
  131.4 1.3 copy.4

commit v4 on v3

--- a/solution.py
+++ b/solution.py
@@ -320,8 +320,7 @@
 FULL = REACH.index(BLOCK)
 FAST_STAGES = len(REACH)
 FIRST = 4
-PLAN = ((0, 0), (1, 0), (2, 0), (4, 4), (4, 5), (0, 1), (1, 1), (2, 1), (4, 6), (4, 7), (0, 2), (1, 2), (2, 2), (0, 3), (1, 3), (2, 3), (0, 4), (0, 5), (2, 4), (1, 4), (3, 3), (0, 6), (2, 5), (1, 5), (3, 5), (0, 7), (2, 6), (1, 6), (1, 7), (2, 7), (3, 7))
-HELD = ()
+PLAN = ((0, 0), (1, 0), (2, 0), (4, 4), (4, 5), (0, 1), (1, 1), (4, 6), (2, 1), (4, 7), (0, 2), (1, 2), (2, 2), (0, 3), (5, 6), (0, 4), (5, 7), (1, 3), (2, 4), (0, 5), (1, 4), (3, 3), (0, 6), (2, 5), (1, 5), (3, 5), (0, 7), (2, 6), (1, 6), (1, 7), (2, 7), (3, 7))
 FAR, ACROSS, PASS, OWN = range(4)
 
 
@@ -338,7 +337,7 @@
 FAST_PIECES = fast_pieces()
 
 
-def fast_kernel(slots, owner, panel, out, *scratch):
+def fast_kernel(slots, source, panel, out, *scratch):
     count = len(FAST_PIECES)
     scratch = list(scratch)
 
@@ -348,7 +347,7 @@
         return taken
 
     ysend, yrecv, zsend, zrecv = take(count), take(count), take(count), take(count)
-    held, high, rest, total, table, local_sem, load_recv, cross_recv, load_send, y_send, f_recv, o_recv, z_send, z_recv = scratch
+    held, high, rest, total, table, owner, owner_sem, local_sem, load_recv, cross_recv, load_send, y_send, f_recv, o_recv, z_send, z_recv = scratch
     per_group = panel.shape[0]
     depth = panel.shape[-1]
     row, col = lax.axis_index("row"), lax.axis_index("col")
@@ -362,6 +361,9 @@
     partners = [sibling, pair, across, opposite, beside]
     halves = range(per_group)
 
+    barrier = pltpu.get_barrier_semaphore()
+    for device in partners:
+        pl.semaphore_signal(barrier, inc=1, device_id=device, device_id_type=MESH)
     fetches = []
     for step in range(STEPS):
         fetch = pltpu.make_async_copy(
@@ -371,9 +373,8 @@
         )
         fetch.start()
         fetches.append(fetch)
-    barrier = pltpu.get_barrier_semaphore()
-    for device in partners:
-        pl.semaphore_signal(barrier, inc=1, device_id=device, device_id_type=MESH)
+    notice = pltpu.make_async_copy(source, owner, owner_sem)
+    notice.start()
     pl.semaphore_wait(barrier, len(partners))
 
     def load_copy(arrivals, step, group, side, device, kind):
@@ -500,27 +501,20 @@
                 ysend[number][index] = product(FAST_PIECES[number][1:], index)
                 y_copy(number, kind, index).start()
 
+    def z_part(stage, slot):
+        for number in numbers(stage):
+            value = product(FAST_PIECES[number][1:], PASS * slots + slot)
+            y_copy(number, FAR, FAR * slots + slot).wait_recv()
+            zsend[number][slot] = value + yrecv[number][FAR * slots + slot]
+            z_copy(number, slot).start()
+
     def z_work(stage):
         @pl.loop(0, slots)
         def _(slot):
-            for number in numbers(stage):
-                value = product(FAST_PIECES[number][1:], PASS * slots + slot)
-                y_copy(number, FAR, FAR * slots + slot).wait_recv()
-                zsend[number][slot] = value + yrecv[number][FAR * slots + slot]
-                if stage in HELD:
-                    @pl.when(h != low)
-                    def _():
-                        z_copy(number, slot).start()
-                else:
-                    z_copy(number, slot).start()
-
-    def release(stage):
-        @pl.when(h == low)
-        def _():
-            for number in numbers(stage):
-                @pl.loop(0, slots)
-                def _(slot):
-                    z_copy(number, slot).start()
+            z_part(stage, slot)
+
+    def z_half(entry):
+        z_part(entry // slots, entry % slots)
 
     def own_work(stage):
         @pl.loop(0, slots)
@@ -548,6 +542,7 @@
 
     for step in range(FIRST):
         begin(step)
+    notice.wait()
     for kind, place in (
         (FAR, (1 - h) * 4 + (1 - low) * 2 + 1 - y),
         (ACROSS, h * 4 + low * 2 + 1 - y),
@@ -575,7 +570,7 @@
     def relay(stage):
         y_work(stage, ACROSS)
 
-    acts = (supply, relay, z_work, own_work, begin, release)
+    acts = (supply, relay, z_work, own_work, begin, z_half)
     for act, argument in PLAN:
         acts[act](argument)
     ready = 0
@@ -617,7 +612,7 @@
     summed = pl.pallas_call(
         functools.partial(fast_kernel, slots),
         out_shape=pltpu.VMEM((slots, BLOCK, BLOCK), jnp.float32),
-        in_specs=[pl.BlockSpec(memory_space=pltpu.SMEM), pl.BlockSpec(memory_space=pl.ANY)],
+        in_specs=[pl.BlockSpec(memory_space=pl.ANY), pl.BlockSpec(memory_space=pl.ANY)],
         out_specs=pl.BlockSpec(memory_space=pltpu.VMEM),
         scratch_shapes=[
             pltpu.VMEM((number, r1 - r0, c1 - c0), jnp.float32)
@@ -630,6 +625,8 @@
             pltpu.VMEM((blocks, BLOCK, 2 * depth), jnp.bfloat16),
             pltpu.VMEM((slots, BLOCK, BLOCK), jnp.float32),
             pltpu.SMEM((3, 4 * slots), jnp.int32),
+            pltpu.SMEM(owner_slot.shape, jnp.int32),
+            pltpu.SemaphoreType.DMA(()),
             pltpu.SemaphoreType.DMA((STEPS,)),
             pltpu.SemaphoreType.DMA((STEPS, 2, 2)),
             pltpu.SemaphoreType.DMA((STEPS, 2, 2)),

time: 133 us -> 132 us (level)
  no operation moved by 1% of the time
where the time goes in v4:
time: 132 us; the launch traced here: 131 us
  Pallas kernels  130 us (98%)
  local copies, waits for them, and re-layouts  1.32 us (1%)
    pallas_call x1, Pallas kernels, quick(): pl.pallas_call(functools.partial(fast_kernel, slots), out_shape=pltpu.VME...  130 us

profile of v4, /device:TPU:19, one launch (start us, length us, event | category | flops | bytes accessed | tf_op | source)
XLA Modules:
  0.0 131.4 jit_solution(5837524682497981217)
XLA Ops:
  0.0 130.1 %shard_map.28 = f32[2,512,512]{2,1,0:T(8,128)S(1)} custom-call(s32[8,8]{1,0:T(8,128)} %source.1, f32[2,512,512]{2,1,0:T(8,128)} %bitcast.3), custom_call_target="tpu_custom_call" | custom-call | flops 4294967296 | bytes 4194304 | tf_op jit(solution)/shard_map/pallas_call | solution.py:612
  130.1 1.3 %copy.4 = f32[1,2,512,512]{3,2,1,0:T(8,128)} copy(f32[1,2,512,512]{3,2,1,0:T(8,128)S(1)} %bitcast.2) | data formatting | bytes 4194304

commit v5 on v4

--- a/solution.py
+++ b/solution.py
@@ -320,7 +320,7 @@
 FULL = REACH.index(BLOCK)
 FAST_STAGES = len(REACH)
 FIRST = 4
-PLAN = ((0, 0), (1, 0), (2, 0), (4, 4), (4, 5), (0, 1), (1, 1), (4, 6), (2, 1), (4, 7), (0, 2), (1, 2), (2, 2), (0, 3), (5, 6), (0, 4), (5, 7), (1, 3), (2, 4), (0, 5), (1, 4), (3, 3), (0, 6), (2, 5), (1, 5), (3, 5), (0, 7), (2, 6), (1, 6), (1, 7), (2, 7), (3, 7))
+PLAN = ((0, 0), (1, 0), (2, 0), (4, 4), (4, 5), (0, 1), (1, 1), (4, 6), (2, 1), (4, 7), (0, 2), (1, 2), (2, 2), (0, 3), (5, 6), (0, 4), (5, 7), (1, 3), (2, 4), (0, 5), (1, 4), (0, 6), (2, 5), (1, 5), (3, 3), (0, 7), (2, 6), (1, 6), (1, 7), (3, 5), (2, 7), (3, 7))
 FAR, ACROSS, PASS, OWN = range(4)
 
 
@@ -478,7 +478,7 @@
             src_ref=ysend[number].at[index],
             dst_ref=yrecv[number].at[index],
             send_sem=y_send,
-            recv_sem=(f_recv.at[number, index] if kind == FAR else o_recv.at[number]),
+            recv_sem=(f_recv.at[number, index] if kind == FAR else o_recv),
             device_id=across,
             device_id_type=MESH,
         )
@@ -526,7 +526,6 @@
     def collect(stage):
         for number in numbers(stage):
             _, r0, r1, c0, c1 = FAST_PIECES[number]
-            y_copy(number, ACROSS, pl.ds(ACROSS * slots, slots)).wait_recv()
             z_copy(number, pl.ds(0, slots)).wait_recv()
 
             @pl.loop(0, slots)
@@ -573,6 +572,10 @@
     acts = (supply, relay, z_work, own_work, begin, z_half)
     for act, argument in PLAN:
         acts[act](argument)
+    whole = held.at[pl.ds(0, slots), 0]
+    pltpu.make_async_remote_copy(
+        src_ref=whole, dst_ref=whole, send_sem=y_send, recv_sem=o_recv, device_id=across, device_id_type=MESH
+    ).wait_recv()
     ready = 0
     for stage in range(FAST_STAGES):
         collect(stage)
@@ -595,7 +598,7 @@
 
     for area, sem in ((held.at[pl.ds(0, slots)], y_send), (held.at[pl.ds(0, slots), 0], z_send)):
         pltpu.make_async_remote_copy(
-            src_ref=area, dst_ref=area, send_sem=sem, recv_sem=o_recv.at[0], device_id=across, device_id_type=MESH
+            src_ref=area, dst_ref=area, send_sem=sem, recv_sem=o_recv, device_id=across, device_id_type=MESH
         ).wait_send()
 
 
@@ -633,7 +636,7 @@
             pltpu.SemaphoreType.DMA((7,)),
             pltpu.SemaphoreType.DMA(()),
             pltpu.SemaphoreType.DMA((count, slots)),
-            pltpu.SemaphoreType.DMA((count,)),
+            pltpu.SemaphoreType.DMA(()),
             pltpu.SemaphoreType.DMA(()),
             pltpu.SemaphoreType.DMA((count,)),
         ],

time: 132 us -> 132 us (level)
  no operation moved by 1% of the time
where the time goes in v5:
time: 132 us; the launch traced here: 131 us
  Pallas kernels  130 us (98%)
  local copies, waits for them, and re-layouts  1.32 us (1%)
    pallas_call x1, Pallas kernels, quick(): pl.pallas_call(functools.partial(fast_kernel, slots), out_shape=pltpu.VME...  130 us

profile of v5, /device:TPU:19, one launch (start us, length us, event | category | flops | bytes accessed | tf_op | source)
XLA Modules:
  0.0 131.3 jit_solution(3688643120144580255)
XLA Ops:
  0.0 130.0 %shard_map.28 = f32[2,512,512]{2,1,0:T(8,128)S(1)} custom-call(s32[8,8]{1,0:T(8,128)} %source.1, f32[2,512,512]{2,1,0:T(8,128)} %bitcast.3), custom_call_target="tpu_custom_call" | custom-call | flops 4294967296 | bytes 4194304 | tf_op jit(solution)/shard_map/pallas_call | solution.py:615
  130.0 1.3 %copy.4 = f32[1,2,512,512]{3,2,1,0:T(8,128)} copy(f32[1,2,512,512]{3,2,1,0:T(8,128)S(1)} %bitcast.2) | data formatting | bytes 4194304
